TPU v7x, 32 devices: a whole 2x2x4 slice. The times are simulated.
32 devices in a mesh: fsdp: 8 (over z, y), tp: 4 (over x, core).
Axes of the slice: x: 2, y: 2, z: 4, core: 2. Of those that a mesh axis runs over, the one named last changes fastest.
Arguments:
- layer_input: bfloat16 [2, 8192, 768], P(None, ('fsdp', 'tp')), may hold values from -6 to 6
- out_grad: bfloat16 [2, 8192, 768], P(None, ('fsdp', 'tp')), may hold values from -6 to 6
- ln1_gain: float32 [768], replicated, may hold values from 0.5 to 1.5
- ln1_bias: float32 [768], replicated, may hold values from -3 to 3
- w_query: bfloat16 [768, 768], P('fsdp', 'tp'), may hold values from -0.21875 to 0.21875
- w_key: bfloat16 [768, 768], P('fsdp', 'tp'), may hold values from -0.21875 to 0.21875
- w_value: bfloat16 [768, 768], P('fsdp', 'tp'), may hold values from -0.21875 to 0.21875
- conv_query: float32 [3, 768], replicated, may hold values from -3 to 3
- conv_key: float32 [3, 768], replicated, may hold values from -3 to 3
- conv_value: float32 [3, 768], replicated, may hold values from -3 to 3
- w_out: bfloat16 [768, 768], P('tp', 'fsdp'), may hold values from -1.25 to 1.25
- ln2_gain: float32 [768], replicated, may hold values from 0.5 to 1.5
- ln2_bias: float32 [768], replicated, may hold values from -3 to 3
- w_up: bfloat16 [768, 3072], P('fsdp', 'tp'), may hold values from -0.21875 to 0.21875
- up_bias: float32 [3072], replicated, may hold values from -3 to 3
- w_down: bfloat16 [3072, 768], P('tp', 'fsdp'), may hold values from -0.109375 to 0.109375
- down_bias: float32 [768], replicated, may hold values from -3 to 3
Outputs:
- layer_out: bfloat16 [2, 8192, 768], P(None, ('fsdp', 'tp'))
- in_grad: bfloat16 [2, 8192, 768], P(None, ('fsdp', 'tp'))
- ln1_gain_grad: float32 [768], replicated
- ln1_bias_grad: float32 [768], replicated
- w_query_grad: float32 [768, 768], P('fsdp', 'tp')
- w_key_grad: float32 [768, 768], P('fsdp', 'tp')
- w_value_grad: float32 [768, 768], P('fsdp', 'tp')
- conv_query_grad: float32 [3, 768], replicated
- conv_key_grad: float32 [3, 768], replicated
- conv_value_grad: float32 [3, 768], replicated
- w_out_grad: float32 [768, 768], P('tp', 'fsdp')
- ln2_gain_grad: float32 [768], replicated
- ln2_bias_grad: float32 [768], replicated
- w_up_grad: float32 [768, 3072], P('fsdp', 'tp')
- up_bias_grad: float32 [3072], replicated
- w_down_grad: float32 [3072, 768], P('tp', 'fsdp')
- down_bias_grad: float32 [768], replicated
All inputs are finite; a program needn't handle non-finite values.
Results may differ from a plain program's by a relative error of at most 0.02.
Values may be sent and summed in bfloat16 or wider, within the bound.
A program may use at most 192 MiB of HBM per device.

v0:
```python
import jax
import jax.numpy as jnp
from jax import lax
from jax.sharding import PartitionSpec as P

HEAD_DIM = 64
D = 768
FF = 3072
KBLOCK = 256
QBLOCK = 512
EPS = 1e-05
MASKED = -1e30


def normalize(values, gain, shift):
    center = values - jnp.mean(values, axis=-1, keepdims=True)
    inverse = lax.rsqrt(jnp.mean(center * center, axis=-1, keepdims=True) + EPS)
    unit = center * inverse
    return (unit, inverse, unit * gain + shift)


def normalize_back(grad_rows, unit, inverse, gain):
    scaled = grad_rows * gain
    return inverse * (
        scaled
        - jnp.mean(scaled, axis=-1, keepdims=True)
        - unit * jnp.mean(scaled * unit, axis=-1, keepdims=True)
    )


def shifted(values, steps):
    return jnp.concatenate(
        [jnp.zeros((steps, values.shape[1]), values.dtype), values[:-steps]], axis=0
    )


def advanced(values, steps):
    return jnp.concatenate(
        [values[steps:], jnp.zeros((steps, values.shape[1]), values.dtype)], axis=0
    )


def conv_apply(values, kernel):
    return kernel[0] * values + kernel[1] * shifted(values, 1) + kernel[2] * shifted(values, 2)


def conv_back(grad_mix, values, kernel):
    grad_values = (
        kernel[0] * grad_mix + kernel[1] * advanced(grad_mix, 1) + kernel[2] * advanced(grad_mix, 2)
    )
    kernel_grad = jnp.stack(
        [
            jnp.sum(grad_mix * values, axis=0),
            jnp.sum(grad_mix * shifted(values, 1), axis=0),
            jnp.sum(grad_mix * shifted(values, 2), axis=0),
        ]
    )
    return (grad_values, kernel_grad)


def block_scores(query_part, key_part, first):
    rows = query_part.shape[0]
    keys = key_part.shape[0]
    row_block = (first + jnp.arange(rows, dtype=jnp.int32)) // KBLOCK
    key_block = jnp.arange(keys, dtype=jnp.int32) // KBLOCK
    allowed = key_block[None, :] <= row_block[:, None]
    raw = jnp.einsum(
        "qhd,khd->hqk", query_part, key_part, preferred_element_type=jnp.float32
    ) * HEAD_DIM ** (-0.5)
    return jnp.where(allowed[None], raw, MASKED)


def attend(query_mix, key_mix, value_mix):
    length = query_mix.shape[0]
    outputs = []
    totals = []
    for first in range(0, length, QBLOCK):
        final = first + QBLOCK
        scores = block_scores(query_mix[first:final], key_mix[:final], first)
        top_score = jnp.max(scores, axis=-1, keepdims=True)
        log_total = top_score + jnp.log(
            jnp.sum(jnp.exp(scores - top_score), axis=-1, keepdims=True)
        )
        weights = jnp.exp(scores - log_total).astype(jnp.bfloat16)
        outputs.append(
            jnp.einsum(
                "hqk,khd->qhd", weights, value_mix[:final], preferred_element_type=jnp.float32
            )
        )
        totals.append(log_total)
    return (jnp.concatenate(outputs, axis=0), totals)


def attend_back(query_mix, key_mix, value_mix, grad_mixed, totals):
    length = query_mix.shape[0]
    grad_query = []
    grad_key = jnp.zeros(key_mix.shape, jnp.float32)
    grad_value = jnp.zeros(value_mix.shape, jnp.float32)
    for number, first in enumerate(range(0, length, QBLOCK)):
        final = first + QBLOCK
        scores = block_scores(query_mix[first:final], key_mix[:final], first)
        exact = jnp.exp(scores - totals[number])
        rounded = exact.astype(jnp.bfloat16)
        grad_weights = jnp.einsum(
            "qhd,khd->hqk",
            grad_mixed[first:final],
            value_mix[:final],
            preferred_element_type=jnp.float32,
        )
        inner = jnp.sum(exact * grad_weights, axis=-1, keepdims=True)
        grad_scores = (exact * (grad_weights - inner)).astype(jnp.bfloat16)
        grad_query.append(
            jnp.einsum(
                "hqk,khd->qhd", grad_scores, key_mix[:final], preferred_element_type=jnp.float32
            )
            * HEAD_DIM ** (-0.5)
        )
        grad_key = grad_key.at[:final].add(
            jnp.einsum(
                "hqk,qhd->khd",
                grad_scores,
                query_mix[first:final],
                preferred_element_type=jnp.float32,
            )
            * HEAD_DIM ** (-0.5)
        )
        grad_value = grad_value.at[:final].add(
            jnp.einsum(
                "hqk,qhd->khd", rounded, grad_mixed[first:final], preferred_element_type=jnp.float32
            )
        )
    return (jnp.concatenate(grad_query, axis=0), grad_key, grad_value)


def fetch(shards):
    return (
        lax.all_gather(shards[0], "fsdp", axis=0, tiled=True),
        lax.all_gather(shards[1], "fsdp", axis=0, tiled=True),
        lax.all_gather(shards[2], "fsdp", axis=0, tiled=True),
        lax.all_gather(shards[3], "fsdp", axis=1, tiled=True),
        lax.all_gather(shards[4], "fsdp", axis=0, tiled=True),
        lax.all_gather(shards[5], "fsdp", axis=1, tiled=True),
    )


def settle(grads):
    return (
        lax.psum_scatter(grads[0], "fsdp", scatter_dimension=0, tiled=True),
        lax.psum_scatter(grads[1], "fsdp", scatter_dimension=0, tiled=True),
        lax.psum_scatter(grads[2], "fsdp", scatter_dimension=0, tiled=True),
        lax.psum_scatter(grads[3], "fsdp", scatter_dimension=1, tiled=True),
        lax.psum_scatter(grads[4], "fsdp", scatter_dimension=0, tiled=True),
        lax.psum_scatter(grads[5], "fsdp", scatter_dimension=1, tiled=True),
    )


def rows_in(piece):
    return lax.all_gather(piece, "tp", axis=0, tiled=True)


def rows_out(term, rows):
    return lax.psum_scatter(
        term(jnp.int32(0), lax.axis_size("tp") * rows).astype(jnp.bfloat16),
        "tp",
        scatter_dimension=0,
        tiled=True,
    ).astype(jnp.float32)


def local(
    layer_input,
    out_grad,
    ln1_gain,
    ln1_bias,
    w_query,
    w_key,
    w_value,
    conv_query,
    conv_key,
    conv_value,
    w_out,
    ln2_gain,
    ln2_bias,
    w_up,
    up_bias,
    w_down,
    down_bias,
):
    rank = lax.axis_index("tp")
    width = w_query.shape[1]
    units = w_up.shape[1]
    heads = width // HEAD_DIM
    kern_query = lax.dynamic_slice_in_dim(conv_query, rank * width, width, 1)
    kern_key = lax.dynamic_slice_in_dim(conv_key, rank * width, width, 1)
    kern_value = lax.dynamic_slice_in_dim(conv_value, rank * width, width, 1)
    bias_up = lax.dynamic_slice_in_dim(up_bias, rank * units, units, 0)
    shards = (w_query, w_key, w_value, w_out, w_up, w_down)
    owned_grads = tuple((jnp.zeros(item.shape, jnp.float32) for item in shards))
    vector_zero = jnp.zeros((D,), jnp.float32)
    gain_one, shift_one, gain_two, shift_two, bias_down_grad = (
        vector_zero,
        vector_zero,
        vector_zero,
        vector_zero,
        vector_zero,
    )
    kernel_zero = jnp.zeros((3, width), jnp.float32)
    query_kernel_grad, key_kernel_grad, value_kernel_grad = (kernel_zero, kernel_zero, kernel_zero)
    bias_up_grad = jnp.zeros((units,), jnp.float32)
    results = []
    input_grads = []
    for micro_step in range(layer_input.shape[0]):
        gathered = fetch(shards)
        full_query, full_key, full_value, full_out, full_up, full_down = gathered
        piece = layer_input[micro_step].astype(jnp.float32)
        rows = piece.shape[0]
        unit_one, inverse_one, normed_one = normalize(piece, ln1_gain, ln1_bias)
        hidden_one = rows_in(normed_one.astype(jnp.bfloat16))
        proj_query = jnp.dot(hidden_one, full_query, preferred_element_type=jnp.float32)
        proj_key = jnp.dot(hidden_one, full_key, preferred_element_type=jnp.float32)
        proj_value = jnp.dot(hidden_one, full_value, preferred_element_type=jnp.float32)
        query_mix = (
            conv_apply(proj_query, kern_query).astype(jnp.bfloat16).reshape(-1, heads, HEAD_DIM)
        )
        key_mix = conv_apply(proj_key, kern_key).astype(jnp.bfloat16).reshape(-1, heads, HEAD_DIM)
        value_mix = (
            conv_apply(proj_value, kern_value).astype(jnp.bfloat16).reshape(-1, heads, HEAD_DIM)
        )
        mixed, totals = attend(query_mix, key_mix, value_mix)
        attn_rows = mixed.reshape(-1, width).astype(jnp.bfloat16)

        def attn_term(start, count):
            return jnp.dot(attn_rows, full_out, preferred_element_type=jnp.float32)

        resid = piece + rows_out(attn_term, rows)
        unit_two, inverse_two, normed_two = normalize(resid, ln2_gain, ln2_bias)
        hidden_two = rows_in(normed_two.astype(jnp.bfloat16))
        pre_act = jnp.dot(hidden_two, full_up, preferred_element_type=jnp.float32) + bias_up
        relu_part = jnp.maximum(pre_act, 0.0)
        activ = (relu_part * relu_part).astype(jnp.bfloat16)

        def ffn_term(start, count):
            return jnp.dot(activ, full_down, preferred_element_type=jnp.float32)

        results.append((resid + rows_out(ffn_term, rows) + down_bias).astype(jnp.bfloat16))
        gathered = fetch(shards)
        full_query, full_key, full_value, full_out, full_up, full_down = gathered
        grad_top = out_grad[micro_step].astype(jnp.float32)
        bias_down_grad = bias_down_grad + jnp.sum(grad_top, axis=0)
        grad_ffn = rows_in(out_grad[micro_step])
        down_local = jnp.einsum("tu,td->ud", activ, grad_ffn, preferred_element_type=jnp.float32)
        grad_act = jnp.einsum("td,ud->tu", grad_ffn, full_down, preferred_element_type=jnp.float32)
        grad_pre = (grad_act * 2.0 * relu_part).astype(jnp.bfloat16)
        bias_up_grad = bias_up_grad + jnp.sum(grad_pre.astype(jnp.float32), axis=0)
        up_local = jnp.einsum("td,tu->du", hidden_two, grad_pre, preferred_element_type=jnp.float32)

        def up_term(start, count):
            return jnp.einsum("tu,du->td", grad_pre, full_up, preferred_element_type=jnp.float32)

        grad_normed_two = rows_out(up_term, rows)
        gain_two = gain_two + jnp.sum(grad_normed_two * unit_two, axis=0)
        shift_two = shift_two + jnp.sum(grad_normed_two, axis=0)
        grad_resid = grad_top + normalize_back(grad_normed_two, unit_two, inverse_two, ln2_gain)
        grad_attn = rows_in(grad_resid.astype(jnp.bfloat16))
        out_local = jnp.einsum(
            "tc,td->cd", attn_rows, grad_attn, preferred_element_type=jnp.float32
        )
        grad_mixed = (
            jnp.einsum("td,cd->tc", grad_attn, full_out, preferred_element_type=jnp.float32)
            .astype(jnp.bfloat16)
            .reshape(-1, heads, HEAD_DIM)
        )
        grad_qmix, grad_kmix, grad_vmix = attend_back(
            query_mix, key_mix, value_mix, grad_mixed, totals
        )
        grad_query, query_tap = conv_back(grad_qmix.reshape(-1, width), proj_query, kern_query)
        grad_key, key_tap = conv_back(grad_kmix.reshape(-1, width), proj_key, kern_key)
        grad_value, value_tap = conv_back(grad_vmix.reshape(-1, width), proj_value, kern_value)
        query_kernel_grad = query_kernel_grad + query_tap
        key_kernel_grad = key_kernel_grad + key_tap
        value_kernel_grad = value_kernel_grad + value_tap
        grad_query = grad_query.astype(jnp.bfloat16)
        grad_key = grad_key.astype(jnp.bfloat16)
        grad_value = grad_value.astype(jnp.bfloat16)
        query_local = jnp.einsum(
            "td,tc->dc", hidden_one, grad_query, preferred_element_type=jnp.float32
        )
        key_local = jnp.einsum(
            "td,tc->dc", hidden_one, grad_key, preferred_element_type=jnp.float32
        )
        value_local = jnp.einsum(
            "td,tc->dc", hidden_one, grad_value, preferred_element_type=jnp.float32
        )

        def input_term(start, count):
            total = jnp.einsum(
                "tc,dc->td", grad_query, full_query, preferred_element_type=jnp.float32
            )
            total = total + jnp.einsum(
                "tc,dc->td", grad_key, full_key, preferred_element_type=jnp.float32
            )
            return total + jnp.einsum(
                "tc,dc->td", grad_value, full_value, preferred_element_type=jnp.float32
            )

        grad_normed_one = rows_out(input_term, rows)
        gain_one = gain_one + jnp.sum(grad_normed_one * unit_one, axis=0)
        shift_one = shift_one + jnp.sum(grad_normed_one, axis=0)
        input_grads.append(
            (grad_resid + normalize_back(grad_normed_one, unit_one, inverse_one, ln1_gain)).astype(
                jnp.bfloat16
            )
        )
        step_grads = (query_local, key_local, value_local, out_local, up_local, down_local)
        owned_grads = jax.tree.map(jnp.add, owned_grads, settle(step_grads))
    kernel_full = jnp.zeros((3, D), jnp.float32)
    query_kernel_full = lax.dynamic_update_slice_in_dim(
        kernel_full, query_kernel_grad, rank * width, 1
    )
    key_kernel_full = lax.dynamic_update_slice_in_dim(kernel_full, key_kernel_grad, rank * width, 1)
    value_kernel_full = lax.dynamic_update_slice_in_dim(
        kernel_full, value_kernel_grad, rank * width, 1
    )
    bias_up_full = lax.dynamic_update_slice_in_dim(
        jnp.zeros((FF,), jnp.float32), bias_up_grad, rank * units, 0
    )
    summed = lax.psum(
        (
            gain_one,
            shift_one,
            query_kernel_full,
            key_kernel_full,
            value_kernel_full,
            gain_two,
            shift_two,
            bias_up_full,
            bias_down_grad,
        ),
        ("fsdp", "tp"),
    )
    return (
        jnp.stack(results),
        jnp.stack(input_grads),
        summed[0],
        summed[1],
        owned_grads[0],
        owned_grads[1],
        owned_grads[2],
        summed[2],
        summed[3],
        summed[4],
        owned_grads[3],
        summed[5],
        summed[6],
        owned_grads[4],
        summed[7],
        owned_grads[5],
        summed[8],
    )


def solution(mesh):
    return jax.shard_map(
        local,
        mesh=mesh,
        in_specs=(
            P(None, ("fsdp", "tp"), None),
            P(None, ("fsdp", "tp"), None),
            P(),
            P(),
            P("fsdp", "tp"),
            P("fsdp", "tp"),
            P("fsdp", "tp"),
            P(),
            P(),
            P(),
            P("tp", "fsdp"),
            P(),
            P(),
            P("fsdp", "tp"),
            P(),
            P("tp", "fsdp"),
            P(),
        ),
        out_specs=(
            P(None, ("fsdp", "tp"), None),
            P(None, ("fsdp", "tp"), None),
            P(),
            P(),
            P("fsdp", "tp"),
            P("fsdp", "tp"),
            P("fsdp", "tp"),
            P(),
            P(),
            P(),
            P("tp", "fsdp"),
            P(),
            P(),
            P("fsdp", "tp"),
            P(),
            P("tp", "fsdp"),
            P(),
        ),
        check_vma=False,
    )
```

profile of v0, /device:TPU:0, one launch (start us, length us, event | category | flops | bytes accessed | tf_op | source)
XLA Modules:
  0.0 1096.2 jit_solution(10316709794128129012)
XLA Ops:
  15.6 35.0 %all_gather.64 = bf16[192,768]{0,1:T(8,128)(2,1)} all-gather(bf16[192,96]{0,1:T(8,128)(2,1)S(1)} %copy.43), channel_id=1, replica_groups=mesh['fsdp'=8,'tp'=4] {'fsdp'}, dimensions={1}, use_global_device_ids=true | all-gather | bytes 331776 | tf_op jit(solution)/shard_map/all_gather | solution.py:140
  50.6 33.2 %all_gather.30 = bf16[768,192]{1,0:T(8,128)(2,1)} all-gather(bf16[96,192]{1,0:T(8,128)(2,1)} %param.45), channel_id=1, replica_groups=mesh['fsdp'=8,'tp'=4] {'fsdp'}, dimensions={0}, use_global_device_ids=true | all-gather | bytes 331776 | tf_op jit(solution)/shard_map/all_gather | solution.py:137
  83.8 31.0 %all_gather.31 = bf16[768,192]{1,0:T(8,128)(2,1)S(1)} all-gather(bf16[96,192]{1,0:T(8,128)(2,1)S(1)} %copy-done.120), channel_id=1, replica_groups=mesh['fsdp'=8,'tp'=4] {'fsdp'}, dimensions={0}, use_global_device_ids=true | all-gather | bytes 331776 | tf_op jit(solution)/shard_map/all_gather | solution.py:138
  114.8 33.2 %all_gather.29 = bf16[768,192]{1,0:T(8,128)(2,1)} all-gather(bf16[96,192]{1,0:T(8,128)(2,1)S(1)} %copy-done.121), channel_id=1, replica_groups=mesh['fsdp'=8,'tp'=4] {'fsdp'}, dimensions={0}, use_global_device_ids=true | all-gather | bytes 331776 | tf_op jit(solution)/shard_map/all_gather | solution.py:139
  165.9 29.3 %reduce-scatter.17.cloned.1.call-done = bf16[256,768]{1,0:T(8,128)(2,1)} async-done(((bf16[1024,768]{1,0:T(8,128)(2,1)}), bf16[256,768]{1,0:T(8,128)(2,1)}) %reduce-scatter.17.cloned.1.call-update) | async-done | bytes 393232 | tf_op jit(solution)/shard_map/reduce_scatter | solution.py:162
  198.2 19.7 %all-gather.21.cloned.1.call-done = bf16[1024,768]{1,0:T(8,128)(2,1)} async-done(((bf16[256,768]{1,0:T(8,128)(2,1)}), bf16[1024,768]{1,0:T(8,128)(2,1)}) %all-gather.21.cloned.1.call-update) | async-done | bytes 1572880 | tf_op jit(solution)/shard_map/all_gather | solution.py:158
  237.3 26.3 %reduce-scatter.21.cloned.1.call-done = bf16[256,768]{1,0:T(8,128)(2,1)} async-done(((bf16[1024,768]{1,0:T(8,128)(2,1)}), bf16[256,768]{1,0:T(8,128)(2,1)}) %reduce-scatter.21.cloned.1.call-update) | async-done | bytes 393232 | tf_op jit(solution)/shard_map/reduce_scatter | solution.py:162
  274.5 4.9 all-gather.17.cloned.1.call-done
  279.4 19.3 %all-gather.23.cloned.1.call-done = bf16[1024,768]{1,0:T(8,128)(2,1)} async-done(((bf16[256,768]{1,0:T(8,128)(2,1)}), bf16[1024,768]{1,0:T(8,128)(2,1)}) %all-gather.23.cloned.1.call-update) | async-done | bytes 1572880 | tf_op jit(solution)/shard_map/all_gather | solution.py:158
  303.5 38.7 %all-gather.19.cloned.1.call-done = bf16[768,768]{0,1:T(8,128)(2,1)} async-done(((bf16[768,96]{0,1:T(8,128)(2,1)}), bf16[768,768]{0,1:T(8,128)(2,1)}) %all-gather.19.cloned.1.call-update) | async-done | bytes 1179664 | tf_op jit(solution)/shard_map/all_gather | solution.py:142
  342.2 19.5 %all-gather.31.cloned.1.call-done = bf16[1,1024,768]{2,1,0:T(8,128)(2,1)} async-done(((bf16[1,256,768]{2,1,0:T(8,128)(2,1)}), bf16[1,1024,768]{2,1,0:T(8,128)(2,1)}) %all-gather.31.cloned.1.call-update) | async-done | bytes 1572880 | tf_op jit(solution)/shard_map/all_gather | solution.py:158
  361.7 4.9 convert_reduce_fusion
  370.4 13.0 %all-gather.15.cloned.1.call-done = bf16[1024,768]{1,0:T(8,128)(2,1)} async-done(((bf16[256,768]{1,0:T(8,128)(2,1)}), bf16[1024,768]{1,0:T(8,128)(2,1)}) %all-gather.15.cloned.1.call-update) | async-done | bytes 1572880 | tf_op jit(solution)/shard_map/all_gather | solution.py:158
  388.2 19.1 %all-gather.29.cloned.1.call-done = bf16[1,1024,768]{2,1,0:T(8,128)(2,1)} async-done(((bf16[1,256,768]{2,1,0:T(8,128)(2,1)}), bf16[1,1024,768]{2,1,0:T(8,128)(2,1)}) %all-gather.29.cloned.1.call-update) | async-done | bytes 1572880 | tf_op jit(solution)/shard_map/all_gather | solution.py:158
  407.2 4.9 convert_reduce_fusion.1
  415.9 28.1 %reduce-scatter.25.cloned.1.call-done = bf16[256,768]{1,0:T(8,128)(2,1)} async-done(((bf16[1024,768]{1,0:T(8,128)(2,1)}), bf16[256,768]{1,0:T(8,128)(2,1)}) %reduce-scatter.25.cloned.1.call-update) | async-done | bytes 393232 | tf_op jit(solution)/shard_map/reduce_scatter | solution.py:162
  451.5 18.6 %all-gather.27.cloned.1.call-done = bf16[1024,768]{1,0:T(8,128)(2,1)} async-done(((bf16[256,768]{1,0:T(8,128)(2,1)}), bf16[1024,768]{1,0:T(8,128)(2,1)}) %all-gather.27.cloned.1.call-update) | async-done | bytes 1572880 | tf_op jit(solution)/shard_map/all_gather | solution.py:158
  481.6 9.9 all-gather.25.cloned.1.call-done
  507.5 5.6 multiply_convert_fusion.4
  522.4 6.3 multiply_reduce_fusion.1
  528.8 7.7 multiply_convert_fusion.1
  573.6 4.8 convolution_convert_fusion.2
  578.5 4.8 convolution_convert_fusion.4
  634.7 16.1 %reduce-scatter.31.cloned.1.call-done = bf16[256,768]{1,0:T(8,128)(2,1)} async-done(((bf16[1024,768]{1,0:T(8,128)(2,1)}), bf16[256,768]{1,0:T(8,128)(2,1)}) %reduce-scatter.31.cloned.1.call-update) | async-done | bytes 393232 | tf_op jit(solution)/shard_map/reduce_scatter | solution.py:162
  650.8 30.4 %reduce-scatter.27.cloned.1.call-done = bf16[256,768]{1,0:T(8,128)(2,1)} async-done(((bf16[1024,768]{1,0:T(8,128)(2,1)}), bf16[256,768]{1,0:T(8,128)(2,1)}) %reduce-scatter.27.cloned.1.call-update) | async-done | bytes 393232 | tf_op jit(solution)/shard_map/reduce_scatter | solution.py:162
  686.7 41.9 %all-reduce.28 = (f32[768]{0:T(1024)}, f32[768]{0:T(1024)}, f32[3,768]{1,0:T(4,128)}, f32[3,768]{1,0:T(4,128)}, f32[3,768]{1,0:T(4,128)}, /*index=5*/f32[768]{0:...) all-reduce(f32[768]{0:T(1024)} %add.555, ...), channel_id=1, replica_groups=mesh['fsdp'=8,'tp'=4] {'fsdp','tp'}, use_global_device_ids=true, to_apply=%region_38.39 | all-reduce | flops 13824 | bytes 110592 | tf_op jit(solution)/shard_map/psum | solution.py:327
  732.9 9.2 reduce-scatter.19.cloned.1.call-done
  745.9 70.2 %reduce-scatter.41.cloned.1.call-done = f32[768,96]{0,1:T(8,128)} async-done(((f32[768,768]{0,1:T(8,128)}), f32[768,96]{0,1:T(8,128)}) %reduce-scatter.41.cloned.1.call-update) | async-done | bytes 294928 | tf_op jit(solution)/shard_map/reduce_scatter | solution.py:153
  816.0 73.3 %reduce-scatter.39.cloned.1.call-done = f32[96,768]{1,0:T(8,128)} async-done(((f32[768,768]{1,0:T(8,128)}), f32[96,768]{1,0:T(8,128)}) %reduce-scatter.39.cloned.1.call-update) | async-done | bytes 294928 | tf_op jit(solution)/shard_map/reduce_scatter | solution.py:152
  889.3 66.4 %reduce-scatter.37.cloned.1.call-done = f32[96,192]{1,0:T(8,128)} async-done(((f32[768,192]{1,0:T(8,128)}), f32[96,192]{1,0:T(8,128)}) %reduce-scatter.37.cloned.1.call-update) | async-done | bytes 73744 | tf_op jit(solution)/shard_map/reduce_scatter | solution.py:150
  955.7 66.3 %reduce-scatter.35.cloned.1.call-done = f32[96,192]{1,0:T(8,128)} async-done(((f32[768,192]{1,0:T(8,128)}), f32[96,192]{1,0:T(8,128)}) %reduce-scatter.35.cloned.1.call-update) | async-done | bytes 73744 | tf_op jit(solution)/shard_map/reduce_scatter | solution.py:149
  1022.0 66.2 %reduce-scatter.33.cloned.1.call-done = f32[96,192]{1,0:T(8,128)} async-done(((f32[768,192]{1,0:T(8,128)}), f32[96,192]{1,0:T(8,128)}) %reduce-scatter.33.cloned.1.call-update) | async-done | bytes 73744 | tf_op jit(solution)/shard_map/reduce_scatter | solution.py:148
  (548 shorter events, 219.9 us)
Async XLA Ops:
  8.0 141.3 %all-gather.13.cloned.1.call-start = ((), (), s32[]{:S(2)}) async-start(), calls=%async_computation.14 | async-start | bytes 1966080 | tf_op jit(solution)/shard_map/all_gather | solution.py:158
  12.7 182.5 %reduce-scatter.17.cloned.1.call-start = ((), (), s32[]{:S(2)}) async-start(), calls=%async_computation.15 | async-start | bytes 1966080 | tf_op jit(solution)/shard_map/reduce_scatter | solution.py:162
  14.6 205.6 %copy-start.143 = (f32[1,192]{1,0:T(1,128)}, f32[1,192]{1,0:T(1,128)S(1)}, u32[]{:S(2)}) copy-start(f32[1,192]{1,0:T(1,128)S(1)} %get-tuple-element.227) | copy-start | bytes 2308
  14.6 205.6 %copy-start.145 = (f32[1,192]{1,0:T(1,128)}, f32[1,192]{1,0:T(1,128)S(1)}, u32[]{:S(2)}) copy-start(f32[1,192]{1,0:T(1,128)S(1)} %get-tuple-element.228) | copy-start | bytes 2308
  15.5 207.5 %copy-start.135 = (f32[1,192]{1,0:T(1,128)}, f32[1,192]{1,0:T(1,128)S(1)}, u32[]{:S(2)}) copy-start(f32[1,192]{1,0:T(1,128)S(1)} %get-tuple-element.255) | copy-start | bytes 2308
  15.5 207.5 %copy-start.137 = (f32[1,192]{1,0:T(1,128)}, f32[1,192]{1,0:T(1,128)S(1)}, u32[]{:S(2)}) copy-start(f32[1,192]{1,0:T(1,128)S(1)} %get-tuple-element.256) | copy-start | bytes 2308
  15.5 207.5 %copy-start.139 = (f32[1,192]{1,0:T(1,128)}, f32[1,192]{1,0:T(1,128)S(1)}, u32[]{:S(2)}) copy-start(f32[1,192]{1,0:T(1,128)S(1)} %get-tuple-element.257) | copy-start | bytes 2308
  15.5 208.9 %copy-start.146 = (f32[1,192]{1,0:T(1,128)}, f32[1,192]{1,0:T(1,128)S(1)}, u32[]{:S(2)}) copy-start(f32[1,192]{1,0:T(1,128)S(1)} %get-tuple-element.232) | copy-start | bytes 2308
  15.6 208.9 %copy-start.147 = (f32[1,192]{1,0:T(1,128)}, f32[1,192]{1,0:T(1,128)S(1)}, u32[]{:S(2)}) copy-start(f32[1,192]{1,0:T(1,128)S(1)} %get-tuple-element.233) | copy-start | bytes 2308
  15.6 208.9 %copy-start.148 = (f32[1,192]{1,0:T(1,128)}, f32[1,192]{1,0:T(1,128)S(1)}, u32[]{:S(2)}) copy-start(f32[1,192]{1,0:T(1,128)S(1)} %get-tuple-element.234) | copy-start | bytes 2308
  165.7 52.2 %all-gather.21.cloned.1.call-start = ((), (), s32[]{:S(2)}) async-start(), calls=%async_computation.20 | async-start | bytes 1966080 | tf_op jit(solution)/shard_map/all_gather | solution.py:158
  198.1 65.5 %reduce-scatter.21.cloned.1.call-start = ((), (), s32[]{:S(2)}) async-start(), calls=%async_computation.21 | async-start | bytes 1966080 | tf_op jit(solution)/shard_map/reduce_scatter | solution.py:162
  235.4 44.0 %all-gather.17.cloned.1.call-start = ((), (), s32[]{:S(2)}) async-start(), calls=%async_computation.17 | async-start | bytes 1327104 | tf_op jit(solution)/shard_map/all_gather | solution.py:141
  236.0 62.7 %all-gather.23.cloned.1.call-start = ((), (), s32[]{:S(2)}) async-start(), calls=%async_computation.22 | async-start | bytes 1966080 | tf_op jit(solution)/shard_map/all_gather | solution.py:158
  268.6 73.6 %all-gather.19.cloned.1.call-start = ((), (), s32[]{:S(2)}) async-start(), calls=%async_computation.18 | async-start | bytes 1327104 | tf_op jit(solution)/shard_map/all_gather | solution.py:142
  269.2 92.5 %all-gather.31.cloned.1.call-start = ((), (), s32[]{:S(2)}) async-start(), calls=%async_computation.31 | async-start | bytes 1966080 | tf_op jit(solution)/shard_map/all_gather | solution.py:158
  271.4 112.0 %all-gather.15.cloned.1.call-start = ((), (), s32[]{:S(2)}) async-start(), calls=%async_computation.16 | async-start | bytes 1966080 | tf_op jit(solution)/shard_map/all_gather | solution.py:158
  272.1 135.1 %all-gather.29.cloned.1.call-start = ((), (), s32[]{:S(2)}) async-start(), calls=%async_computation.30 | async-start | bytes 1966080 | tf_op jit(solution)/shard_map/all_gather | solution.py:158
  272.9 143.1 %reduce-scatter.29.cloned.1.call-start = ((), (), s32[]{:S(2)}) async-start(), calls=%async_computation.27 | async-start | bytes 1966080 | tf_op jit(solution)/shard_map/reduce_scatter | solution.py:162
  370.4 73.7 %reduce-scatter.25.cloned.1.call-start = ((), (), s32[]{:S(2)}) async-start(), calls=%async_computation.24 | async-start | bytes 1966080 | tf_op jit(solution)/shard_map/reduce_scatter | solution.py:162
  415.9 54.2 %all-gather.27.cloned.1.call-start = ((), (), s32[]{:S(2)}) async-start(), calls=%async_computation.28 | async-start | bytes 1966080 | tf_op jit(solution)/shard_map/all_gather | solution.py:158
  450.4 41.1 %all-gather.25.cloned.1.call-start = ((), (), s32[]{:S(2)}) async-start(), calls=%async_computation.25 | async-start | bytes 1966080 | tf_op jit(solution)/shard_map/all_gather | solution.py:158
  451.0 182.0 %reduce-scatter.43.cloned.1.call-start = ((), (), s32[]{:S(2)}) async-start(), calls=%async_computation.37 | async-start | bytes 884736
  557.7 93.1 %reduce-scatter.31.cloned.1.call-start = ((), (), s32[]{:S(2)}) async-start(), calls=%async_computation.29 | async-start | bytes 1966080 | tf_op jit(solution)/shard_map/reduce_scatter | solution.py:162
  569.0 112.2 %reduce-scatter.27.cloned.1.call-start = ((), (), s32[]{:S(2)}) async-start(), calls=%async_computation.26 | async-start | bytes 1966080 | tf_op jit(solution)/shard_map/reduce_scatter | solution.py:162
  573.6 156.4 %reduce-scatter.23.cloned.1.call-start = ((), (), s32[]{:S(2)}) async-start(), calls=%async_computation.23 | async-start | bytes 1966080 | tf_op jit(solution)/shard_map/reduce_scatter | solution.py:162
  578.5 163.7 %reduce-scatter.19.cloned.1.call-start = ((), (), s32[]{:S(2)}) async-start(), calls=%async_computation.19 | async-start | bytes 1966080 | tf_op jit(solution)/shard_map/reduce_scatter | solution.py:162
  583.4 232.7 %reduce-scatter.41.cloned.1.call-start = ((), (), s32[]{:S(2)}) async-start(), calls=%async_computation.36 | async-start | bytes 2654208 | tf_op jit(solution)/shard_map/reduce_scatter | solution.py:153
  590.6 298.7 %reduce-scatter.39.cloned.1.call-start = ((), (), s32[]{:S(2)}) async-start(), calls=%async_computation.35 | async-start | bytes 2654208 | tf_op jit(solution)/shard_map/reduce_scatter | solution.py:152
  597.4 358.3 %reduce-scatter.37.cloned.1.call-start = ((), (), s32[]{:S(2)}) async-start(), calls=%async_computation.34 | async-start | bytes 884736 | tf_op jit(solution)/shard_map/reduce_scatter | solution.py:150
  608.7 413.3 %reduce-scatter.35.cloned.1.call-start = ((), (), s32[]{:S(2)}) async-start(), calls=%async_computation.33 | async-start | bytes 884736 | tf_op jit(solution)/shard_map/reduce_scatter | solution.py:149
  620.9 467.3 %reduce-scatter.33.cloned.1.call-start = ((), (), s32[]{:S(2)}) async-start(), calls=%async_computation.32 | async-start | bytes 884736 | tf_op jit(solution)/shard_map/reduce_scatter | solution.py:148
  (158 other events, 2125.6 us)
Sparse Core Ops, SparseCore 0:
  12.8 22.3 all-gather.12
  165.8 29.3 reduce-scatter.16
  198.2 19.6 all-gather.20
  235.5 28.0 reduce-scatter.20
  370.5 28.3 reduce-scatter.28
  416.0 27.9 reduce-scatter.24
Sparse Core Ops, SparseCore 1:
  238.1 41.3 all-gather.16
  280.9 17.8 all-gather.22
  300.8 41.4 all-gather.18
  343.8 17.8 all-gather.30
  363.9 19.5 all-gather.14
  385.0 22.2 all-gather.28
  450.5 19.5 all-gather.26
  472.0 19.5 all-gather.24
  557.8 63.4 reduce-scatter.42
  623.8 26.9 reduce-scatter.30
  653.3 27.9 reduce-scatter.26
  683.8 28.0 reduce-scatter.22
  714.3 27.8 reduce-scatter.18
  746.3 69.7 reduce-scatter.40
  820.1 69.1 reduce-scatter.38
  893.2 62.4 reduce-scatter.36
  959.6 62.3 reduce-scatter.34
  1025.9 62.3 reduce-scatter.32
where the time goes:
time: 1110 us; the launch traced here: 1100 us
  waiting for transfers between devices  648 us (58%)
  blocking collectives  174 us (16%)
  matrix products  132 us (12%)
  other arithmetic  90.4 us (8%)
  local copies, waits for them, and re-layouts  30.4 us (3%)
  between operations  18.5 us (2%)
    reduce_scatter x8, waiting for transfers between devices, rows_out(): lax.psum_scatter(term(jnp.int32(0), lax.axis_size('tp') * rows).astype(jn...  139 us
    all_gather x8, waiting for transfers between devices, rows_in(): return lax.all_gather(piece, 'tp', axis=0, tiled=True)  119 us
    reduce_scatter x1, waiting for transfers between devices, settle(): lax.psum_scatter(grads[4], 'fsdp', scatter_dimension=0, tiled=True)  73.3 us
    reduce_scatter x1, waiting for transfers between devices, settle(): lax.psum_scatter(grads[5], 'fsdp', scatter_dimension=1, tiled=True)  70.2 us
    reduce_scatter x1, waiting for transfers between devices, settle(): lax.psum_scatter(grads[2], 'fsdp', scatter_dimension=0, tiled=True)  66.4 us
    reduce_scatter x1, waiting for transfers between devices, settle(): lax.psum_scatter(grads[1], 'fsdp', scatter_dimension=0, tiled=True)  66.3 us
    reduce_scatter x1, waiting for transfers between devices, settle(): lax.psum_scatter(grads[0], 'fsdp', scatter_dimension=0, tiled=True)  66.2 us
    psum x1, blocking collectives, local(): lax.psum((gain_one, shift_one, query_kernel_full, key_kernel_full, value_...  41.9 us
  transfers between devices with their start and end apart: 24, of which 20 were waited for; matrix products, arithmetic and copies ran while one was open for 12% of the time, Pallas kernels for 0%

commit v1 on v0

--- a/solution.py
+++ b/solution.py
@@ -10,6 +10,24 @@
 QBLOCK = 512
 EPS = 1e-05
 MASKED = -1e30
+
+
+def ring_gather(array, axis, dim):
+    ways, here, hop = (lax.axis_size(axis), lax.axis_index(axis), array.shape[dim])
+    dims = [n * ways if d == dim else n for d, n in enumerate(array.shape)]
+    full = lax.dynamic_update_slice_in_dim(
+        jnp.zeros(dims, array.dtype), array, here * hop, axis=dim
+    )
+    going_up = going_down = array
+    for far in range(1, ways // 2 + 1):
+        going_up = lax.ppermute(going_up, axis, [(d, (d + 1) % ways) for d in range(ways)])
+        full = lax.dynamic_update_slice_in_dim(full, going_up, (here - far) % ways * hop, axis=dim)
+        if 2 * far < ways:
+            going_down = lax.ppermute(going_down, axis, [(d, (d - 1) % ways) for d in range(ways)])
+            full = lax.dynamic_update_slice_in_dim(
+                full, going_down, (here + far) % ways * hop, axis=dim
+            )
+    return full
 
 
 def normalize(values, gain, shift):
@@ -155,7 +173,7 @@
 
 
 def rows_in(piece):
-    return lax.all_gather(piece, "tp", axis=0, tiled=True)
+    return ring_gather(piece, "tp", 0)
 
 
 def rows_out(term, rows):

time: 1110 us -> 1040 us (0.937)
  waiting for transfers between devices: 648 us -> 583 us
  matrix products: 132 us -> 113 us
  local copies, waits for them, and re-layouts: 30.4 us -> 46.1 us
  starting transfers between devices: 2.57 us -> 17.3 us
    all_gather x8 -> x0, waiting for transfers between devices: 119 us -> none  [rows_in(): return lax.all_gather(piece, 'tp', axis=0, tiled=True)]
    ppermute x0 -> x24, waiting for transfers between devices: none -> 78.4 us  [the longest x16 76.3 us: ring_gather(): lax.ppermute(going_up, axis, [(d, (d + 1) % ways) for d in range(ways)])]
    all_gather x1, waiting for transfers between devices: 38.7 us -> 21.5 us  [fetch(): lax.all_gather(shards[5], 'fsdp', axis=1, tiled=True)]
    ppermute x0 -> x24, starting transfers between devices: none -> 15.8 us  [the longest x8 10.9 us: ring_gather(): lax.ppermute(going_down, axis, [(d, (d - 1) % ways) for d in range(ways)])]
    dynamic_update_slice x0 -> x26, local copies, waits for them, and re-layouts: none -> 12.2 us  [the longest x16 7.64 us: ring_gather(): lax.dynamic_update_slice_in_dim(full, going_up, (here - far) % ways * hop...]
  transfers between devices with their start and end apart: 24 -> 40, of which waited for: 20 -> 27; matrix products, arithmetic and copies ran while one was open for 12% -> 12% of each run, Pallas kernels for 0% -> 0%
where the time goes in v1:
time: 1040 us; the launch traced here: 1030 us
  waiting for transfers between devices  583 us (56%)
  blocking collectives  170 us (16%)
  matrix products  113 us (11%)
  other arithmetic  85.8 us (8%)
  local copies, waits for them, and re-layouts  46.1 us (4%)
  between operations  18.5 us (2%)
  starting transfers between devices  17.3 us (2%)
    reduce_scatter x8, waiting for transfers between devices, rows_out(): lax.psum_scatter(term(jnp.int32(0), lax.axis_size('tp') * rows).astype(jn...  140 us
    ppermute x16, waiting for transfers between devices, ring_gather(): lax.ppermute(going_up, axis, [(d, (d + 1) % ways) for d in range(ways)])  76.3 us
    reduce_scatter x1, waiting for transfers between devices, settle(): lax.psum_scatter(grads[4], 'fsdp', scatter_dimension=0, tiled=True)  72.9 us
    reduce_scatter x1, waiting for transfers between devices, settle(): lax.psum_scatter(grads[5], 'fsdp', scatter_dimension=1, tiled=True)  70 us
    reduce_scatter x1, waiting for transfers between devices, settle(): lax.psum_scatter(grads[2], 'fsdp', scatter_dimension=0, tiled=True)  66.3 us
    reduce_scatter x1, waiting for transfers between devices, settle(): lax.psum_scatter(grads[0], 'fsdp', scatter_dimension=0, tiled=True)  66.2 us
    reduce_scatter x1, waiting for transfers between devices, settle(): lax.psum_scatter(grads[1], 'fsdp', scatter_dimension=0, tiled=True)  66.1 us
    psum x1, blocking collectives, local(): lax.psum((gain_one, shift_one, query_kernel_full, key_kernel_full, value_...  41.6 us
  transfers between devices with their start and end apart: 40, of which 27 were waited for; matrix products, arithmetic and copies ran while one was open for 12% of the time, Pallas kernels for 0%

profile of v1, /device:TPU:0, one launch (start us, length us, event | category | flops | bytes accessed | tf_op | source)
XLA Modules:
  0.0 1032.6 jit_solution(2704675430273110538)
XLA Ops:
  16.1 32.3 %all_gather.15 = bf16[192,768]{0,1:T(8,128)(2,1)S(1)} all-gather(bf16[192,96]{0,1:T(8,128)(2,1)S(1)} %copy.43), channel_id=1, replica_groups=mesh['fsdp'=8,'tp'=4] {'fsdp'}, dimensions={1}, use_global_device_ids=true | all-gather | bytes 331776 | tf_op jit(solution)/shard_map/all_gather | solution.py:158
  48.4 33.1 %all_gather.13 = bf16[768,192]{1,0:T(8,128)(2,1)} all-gather(bf16[96,192]{1,0:T(8,128)(2,1)S(1)} %copy-done.117), channel_id=1, replica_groups=mesh['fsdp'=8,'tp'=4] {'fsdp'}, dimensions={0}, use_global_device_ids=true | all-gather | bytes 331776 | tf_op jit(solution)/shard_map/all_gather | solution.py:155
  81.6 31.0 %all_gather.14 = bf16[768,192]{1,0:T(8,128)(2,1)S(1)} all-gather(bf16[96,192]{1,0:T(8,128)(2,1)S(1)} %copy-done.118), channel_id=1, replica_groups=mesh['fsdp'=8,'tp'=4] {'fsdp'}, dimensions={0}, use_global_device_ids=true | all-gather | bytes 331776 | tf_op jit(solution)/shard_map/all_gather | solution.py:156
  116.0 31.8 %all_gather.12 = bf16[768,192]{1,0:T(8,128)(2,1)S(1)} all-gather(bf16[96,192]{1,0:T(8,128)(2,1)} %param.47), channel_id=1, replica_groups=mesh['fsdp'=8,'tp'=4] {'fsdp'}, dimensions={0}, use_global_device_ids=true | all-gather | bytes 331776 | tf_op jit(solution)/shard_map/all_gather | solution.py:157
  165.2 29.2 %reduce-scatter.17.cloned.1.call-done = bf16[256,768]{1,0:T(8,128)(2,1)} async-done(((bf16[1024,768]{1,0:T(8,128)(2,1)}), bf16[256,768]{1,0:T(8,128)(2,1)}) %reduce-scatter.17.cloned.1.call-update) | async-done | bytes 393232 | tf_op jit(solution)/shard_map/reduce_scatter | solution.py:180
  199.1 9.0 collective-permute-done.6
  208.4 7.1 collective-permute-done.8
  232.3 25.7 %reduce-scatter.21.cloned.1.call-done = bf16[256,768]{1,0:T(8,128)(2,1)} async-done(((bf16[1024,768]{1,0:T(8,128)(2,1)}), bf16[256,768]{1,0:T(8,128)(2,1)}) %reduce-scatter.21.cloned.1.call-update) | async-done | bytes 393232 | tf_op jit(solution)/shard_map/reduce_scatter | solution.py:180
  277.8 6.1 collective-permute-done.20
  289.5 4.7 fusion.123
  294.3 21.5 %all-gather.5.cloned.1.call-done = bf16[768,768]{0,1:T(8,128)(2,1)} async-done(((bf16[768,96]{0,1:T(8,128)(2,1)}), bf16[768,768]{0,1:T(8,128)(2,1)}) %all-gather.5.cloned.1.call-update) | async-done | bytes 1179664 | tf_op jit(solution)/shard_map/all_gather | solution.py:160
  315.8 4.9 convert_reduce_fusion
  334.5 6.4 collective-permute-done.3
  342.5 14.2 %collective-permute-done.14 = bf16[256,768]{1,0:T(8,128)(2,1)S(1)} collective-permute-done((bf16[256,768]{1,0:T(8,128)(2,1)S(1)}, bf16[256,768]{1,0:T(8,128)(2,1)S(1)}, u32[]{:S(2)}, u32[]{:S(2)}) %collective-permute-start.14) | collective-permute-done | bytes 393248 | tf_op jit(solution)/shard_map/ppermute | solution.py:23
  356.9 4.6 collective-permute-done.5
  370.2 26.4 %reduce-scatter.25.cloned.1.call-done = bf16[256,768]{1,0:T(8,128)(2,1)} async-done(((bf16[1024,768]{1,0:T(8,128)(2,1)}), bf16[256,768]{1,0:T(8,128)(2,1)}) %reduce-scatter.25.cloned.1.call-update) | async-done | bytes 393232 | tf_op jit(solution)/shard_map/reduce_scatter | solution.py:180
  403.0 7.0 collective-permute-done.21
  410.0 8.4 collective-permute-done.15
  444.6 6.8 multiply_convert_fusion.4
  460.6 6.3 multiply_reduce_fusion.1
  467.0 7.6 multiply_convert_fusion.1
  511.9 4.9 convolution_convert_fusion.2
  516.9 4.5 convolution_convert_fusion.4
  572.2 16.0 %reduce-scatter.27.cloned.1.call-done = bf16[256,768]{1,0:T(8,128)(2,1)} async-done(((bf16[1024,768]{1,0:T(8,128)(2,1)}), bf16[256,768]{1,0:T(8,128)(2,1)}) %reduce-scatter.27.cloned.1.call-update) | async-done | bytes 393232 | tf_op jit(solution)/shard_map/reduce_scatter | solution.py:180
  588.2 30.5 %reduce-scatter.31.cloned.1.call-done = bf16[256,768]{1,0:T(8,128)(2,1)} async-done(((bf16[1024,768]{1,0:T(8,128)(2,1)}), bf16[256,768]{1,0:T(8,128)(2,1)}) %reduce-scatter.31.cloned.1.call-update) | async-done | bytes 393232 | tf_op jit(solution)/shard_map/reduce_scatter | solution.py:180
  622.5 41.6 %all-reduce.28 = (f32[768]{0:T(1024)}, f32[768]{0:T(1024)}, f32[3,768]{1,0:T(4,128)}, f32[3,768]{1,0:T(4,128)}, f32[3,768]{1,0:T(4,128)}, /*index=5*/f32[768]{0:...) all-reduce(f32[768]{0:T(1024)S(1)} %add.646, ...), channel_id=1, replica_groups=mesh['fsdp'=8,'tp'=4] {'fsdp','tp'}, use_global_device_ids=true, to_apply=%region_38.39 | all-reduce | flops 13824 | bytes 110592 | tf_op jit(solution)/shard_map/psum | solution.py:345
  667.4 12.3 %reduce-scatter.19.cloned.1.call-done = bf16[256,768]{1,0:T(8,128)(2,1)} async-done(((bf16[1024,768]{1,0:T(8,128)(2,1)}), bf16[256,768]{1,0:T(8,128)(2,1)}) %reduce-scatter.19.cloned.1.call-update) | async-done | bytes 393232 | tf_op jit(solution)/shard_map/reduce_scatter | solution.py:180
  683.4 70.0 %reduce-scatter.41.cloned.1.call-done = f32[768,96]{0,1:T(8,128)} async-done(((f32[768,768]{0,1:T(8,128)}), f32[768,96]{0,1:T(8,128)}) %reduce-scatter.41.cloned.1.call-update) | async-done | bytes 294928 | tf_op jit(solution)/shard_map/reduce_scatter | solution.py:171
  753.4 72.9 %reduce-scatter.39.cloned.1.call-done = f32[96,768]{1,0:T(8,128)} async-done(((f32[768,768]{1,0:T(8,128)}), f32[96,768]{1,0:T(8,128)}) %reduce-scatter.39.cloned.1.call-update) | async-done | bytes 294928 | tf_op jit(solution)/shard_map/reduce_scatter | solution.py:170
  826.3 66.3 %reduce-scatter.37.cloned.1.call-done = f32[96,192]{1,0:T(8,128)} async-done(((f32[768,192]{1,0:T(8,128)}), f32[96,192]{1,0:T(8,128)}) %reduce-scatter.37.cloned.1.call-update) | async-done | bytes 73744 | tf_op jit(solution)/shard_map/reduce_scatter | solution.py:168
  892.7 66.1 %reduce-scatter.35.cloned.1.call-done = f32[96,192]{1,0:T(8,128)} async-done(((f32[768,192]{1,0:T(8,128)}), f32[96,192]{1,0:T(8,128)}) %reduce-scatter.35.cloned.1.call-update) | async-done | bytes 73744 | tf_op jit(solution)/shard_map/reduce_scatter | solution.py:167
  958.8 66.2 %reduce-scatter.33.cloned.1.call-done = f32[96,192]{1,0:T(8,128)} async-done(((f32[768,192]{1,0:T(8,128)}), f32[96,192]{1,0:T(8,128)}) %reduce-scatter.33.cloned.1.call-update) | async-done | bytes 73744 | tf_op jit(solution)/shard_map/reduce_scatter | solution.py:166
  (636 shorter events, 238.3 us)
Async XLA Ops:
  8.1 186.3 %reduce-scatter.17.cloned.1.call-start = ((), (), s32[]{:S(2)}) async-start(), calls=%async_computation.14 | async-start | bytes 1966080 | tf_op jit(solution)/shard_map/reduce_scatter | solution.py:180
  13.4 101.1 %collective-permute-start = (bf16[256,768]{1,0:T(8,128)(2,1)}, bf16[256,768]{1,0:T(8,128)(2,1)}, u32[]{:S(2)}, u32[]{:S(2)}) collective-permute-start(bf16[256,768]{1,0:T(8,128)(2,1)} %get-tuple-element.215), channel_id=1, source_target_pairs={{0,1},{1,2},{2,3},{3,0},{4,5},{5,6},{6,7},{7,4},{8,9},{9,10},{10,1... | collective-permute-start | bytes 1179656 | tf_op jit(solution)/shard_map/ppermute | solution.py:23
  13.9 135.1 %collective-permute-start.1 = (bf16[256,768]{1,0:T(8,128)(2,1)}, bf16[256,768]{1,0:T(8,128)(2,1)}, u32[]{:S(2)}, u32[]{:S(2)}) collective-permute-start(bf16[256,768]{1,0:T(8,128)(2,1)} %get-tuple-element.215), channel_id=1, source_target_pairs={{0,3},{1,0},{2,1},{3,2},{4,7},{5,4},{6,5},{7,6},{8,11},{9,8},{10,9... | collective-permute-start | bytes 1179656 | tf_op jit(solution)/shard_map/ppermute | solution.py:26
  114.4 35.6 %collective-permute-start.2 = (bf16[256,768]{1,0:T(8,128)(2,1)}, bf16[256,768]{1,0:T(8,128)(2,1)}, u32[]{:S(2)}, u32[]{:S(2)}) collective-permute-start(bf16[256,768]{1,0:T(8,128)(2,1)} %collective-permute-done), channel_id=1, source_target_pairs={{0,1},{1,2},{2,3},{3,0},{4,5},{5,6},{6,7},{7,4},{8,9},{9,10},{10,1... | collective-permute-start | bytes 1179656 | tf_op jit(solution)/shard_map/ppermute | solution.py:23
  165.1 93.0 %reduce-scatter.21.cloned.1.call-start = ((), (), s32[]{:S(2)}) async-start(), calls=%async_computation.18 | async-start | bytes 1966080 | tf_op jit(solution)/shard_map/reduce_scatter | solution.py:180
  230.2 59.4 %all-gather.3.cloned.1.call-start = ((), (), s32[]{:S(2)}) async-start(), calls=%async_computation.15 | async-start | bytes 1327104 | tf_op jit(solution)/shard_map/all_gather | solution.py:159
  230.8 85.1 %all-gather.5.cloned.1.call-start = ((), (), s32[]{:S(2)}) async-start(), calls=%async_computation.16 | async-start | bytes 1327104 | tf_op jit(solution)/shard_map/all_gather | solution.py:160
  231.7 35.9 %collective-permute-start.18 = (bf16[256,768]{1,0:T(8,128)(2,1)}, bf16[256,768]{1,0:T(8,128)(2,1)}, u32[]{:S(2)}, u32[]{:S(2)}) collective-permute-start(bf16[256,768]{1,0:T(8,128)(2,1)} %get-tuple-element.220), channel_id=1, source_target_pairs={{0,1},{1,2},{2,3},{3,0},{4,5},{5,6},{6,7},{7,4},{8,9},{9,10},{10,1... | collective-permute-start | bytes 1179656 | tf_op jit(solution)/shard_map/ppermute | solution.py:23
  231.8 138.4 %reduce-scatter.29.cloned.1.call-start = ((), (), s32[]{:S(2)}) async-start(), calls=%async_computation.22 | async-start | bytes 1966080 | tf_op jit(solution)/shard_map/reduce_scatter | solution.py:180
  267.6 16.3 %collective-permute-start.20 = (bf16[256,768]{1,0:T(8,128)(2,1)}, bf16[256,768]{1,0:T(8,128)(2,1)S(1)}, u32[]{:S(2)}, u32[]{:S(2)}) collective-permute-start(bf16[256,768]{1,0:T(8,128)(2,1)} %collective-permute-done.18), channel_id=1, source_target_pairs={{0,1},{1,2},{2,3},{3,0},{4,5},{5,6},{6,7},{7,4},{8,9},{9,10},{10,1... | collective-permute-start | bytes 1179656 | tf_op jit(solution)/shard_map/ppermute | solution.py:23
  269.7 16.8 %collective-permute-start.10 = (bf16[256,768]{1,0:T(8,128)(2,1)}, bf16[256,768]{1,0:T(8,128)(2,1)S(1)}, u32[]{:S(2)}, u32[]{:S(2)}) collective-permute-start(bf16[256,768]{1,0:T(8,128)(2,1)} %get-tuple-element.211), channel_id=1, source_target_pairs={{0,3},{1,0},{2,1},{3,2},{4,7},{5,4},{6,5},{7,6},{8,11},{9,8},{10,9... | collective-permute-start | bytes 1179656 | tf_op jit(solution)/shard_map/ppermute | solution.py:26
  275.6 13.2 %collective-permute-start.11 = (bf16[256,768]{1,0:T(8,128)(2,1)}, bf16[256,768]{1,0:T(8,128)(2,1)S(1)}, u32[]{:S(2)}, u32[]{:S(2)}) collective-permute-start(bf16[256,768]{1,0:T(8,128)(2,1)} %collective-permute-done.9), channel_id=1, source_target_pairs={{0,1},{1,2},{2,3},{3,0},{4,5},{5,6},{6,7},{7,4},{8,9},{9,10},{10,1... | collective-permute-start | bytes 1179656 | tf_op jit(solution)/shard_map/ppermute | solution.py:23
  324.5 72.1 %reduce-scatter.25.cloned.1.call-start = ((), (), s32[]{:S(2)}) async-start(), calls=%async_computation.20 | async-start | bytes 1966080 | tf_op jit(solution)/shard_map/reduce_scatter | solution.py:180
  326.8 14.2 %collective-permute-start.3 = (bf16[256,768]{1,0:T(8,128)(2,1)S(1)}, bf16[256,768]{1,0:T(8,128)(2,1)S(1)}, u32[]{:S(2)}, u32[]{:S(2)}) collective-permute-start(bf16[256,768]{1,0:T(8,128)(2,1)S(1)} %get-tuple-element.209), channel_id=1, source_target_pairs={{0,1},{1,2},{2,3},{3,0},{4,5},{5,6},{6,7},{7,4},{8,9},{9,10},{10,1... | collective-permute-start | bytes 1179656 | tf_op jit(solution)/shard_map/ppermute | solution.py:23
  328.3 14.2 %collective-permute-start.13 = (bf16[256,768]{1,0:T(8,128)(2,1)S(1)}, bf16[256,768]{1,0:T(8,128)(2,1)S(1)}, u32[]{:S(2)}, u32[]{:S(2)}) collective-permute-start(bf16[256,768]{1,0:T(8,128)(2,1)S(1)} %copy-done.108), channel_id=1, source_target_pairs={{0,3},{1,0},{2,1},{3,2},{4,7},{5,4},{6,5},{7,6},{8,11},{9,8},{10,9... | collective-permute-start | bytes 1179656 | tf_op jit(solution)/shard_map/ppermute | solution.py:26
  332.5 24.2 %collective-permute-start.14 = (bf16[256,768]{1,0:T(8,128)(2,1)S(1)}, bf16[256,768]{1,0:T(8,128)(2,1)S(1)}, u32[]{:S(2)}, u32[]{:S(2)}) collective-permute-start(bf16[256,768]{1,0:T(8,128)(2,1)S(1)} %collective-permute-done.12), channel_id=1, source_target_pairs={{0,1},{1,2},{2,3},{3,0},{4,5},{5,6},{6,7},{7,4},{8,9},{9,10},{10,1... | collective-permute-start | bytes 1179656 | tf_op jit(solution)/shard_map/ppermute | solution.py:23
  332.8 24.1 %collective-permute-start.4 = (bf16[256,768]{1,0:T(8,128)(2,1)S(1)}, bf16[256,768]{1,0:T(8,128)(2,1)S(1)}, u32[]{:S(2)}, u32[]{:S(2)}) collective-permute-start(bf16[256,768]{1,0:T(8,128)(2,1)S(1)} %get-tuple-element.209), channel_id=1, source_target_pairs={{0,3},{1,0},{2,1},{3,2},{4,7},{5,4},{6,5},{7,6},{8,11},{9,8},{10,9... | collective-permute-start | bytes 1179656 | tf_op jit(solution)/shard_map/ppermute | solution.py:26
  341.0 20.6 %collective-permute-start.5 = (bf16[256,768]{1,0:T(8,128)(2,1)S(1)}, bf16[256,768]{1,0:T(8,128)(2,1)S(1)}, u32[]{:S(2)}, u32[]{:S(2)}) collective-permute-start(bf16[256,768]{1,0:T(8,128)(2,1)S(1)} %collective-permute-done.3), channel_id=1, source_target_pairs={{0,1},{1,2},{2,3},{3,0},{4,5},{5,6},{6,7},{7,4},{8,9},{9,10},{10,1... | collective-permute-start | bytes 1179656 | tf_op jit(solution)/shard_map/ppermute | solution.py:23
  370.1 200.4 %reduce-scatter.43.cloned.1.call-start = ((), (), s32[]{:S(2)}) async-start(), calls=%async_computation.29 | async-start | bytes 884736
  401.0 17.5 %collective-permute-start.15 = (bf16[256,768]{1,0:T(8,128)(2,1)S(1)}, bf16[256,768]{1,0:T(8,128)(2,1)S(1)}, u32[]{:S(2)}, u32[]{:S(2)}) collective-permute-start(bf16[256,768]{1,0:T(8,128)(2,1)S(1)} %get-tuple-element.205), channel_id=1, source_target_pairs={{0,1},{1,2},{2,3},{3,0},{4,5},{5,6},{6,7},{7,4},{8,9},{9,10},{10,1... | collective-permute-start | bytes 1179656 | tf_op jit(solution)/shard_map/ppermute | solution.py:23
  401.2 17.6 %collective-permute-start.22 = (bf16[256,768]{1,0:T(8,128)(2,1)S(1)}, bf16[256,768]{1,0:T(8,128)(2,1)S(1)}, u32[]{:S(2)}, u32[]{:S(2)}) collective-permute-start(bf16[256,768]{1,0:T(8,128)(2,1)S(1)} %get-tuple-element.207), channel_id=1, source_target_pairs={{0,3},{1,0},{2,1},{3,2},{4,7},{5,4},{6,5},{7,6},{8,11},{9,8},{10,9... | collective-permute-start | bytes 1179656 | tf_op jit(solution)/shard_map/ppermute | solution.py:26
  402.8 17.9 %collective-permute-start.16 = (bf16[256,768]{1,0:T(8,128)(2,1)S(1)}, bf16[256,768]{1,0:T(8,128)(2,1)S(1)}, u32[]{:S(2)}, u32[]{:S(2)}) collective-permute-start(bf16[256,768]{1,0:T(8,128)(2,1)S(1)} %get-tuple-element.205), channel_id=1, source_target_pairs={{0,3},{1,0},{2,1},{3,2},{4,7},{5,4},{6,5},{7,6},{8,11},{9,8},{10,9... | collective-permute-start | bytes 1179656 | tf_op jit(solution)/shard_map/ppermute | solution.py:26
  410.0 14.2 %collective-permute-start.23 = (bf16[256,768]{1,0:T(8,128)(2,1)S(1)}, bf16[256,768]{1,0:T(8,128)(2,1)S(1)}, u32[]{:S(2)}, u32[]{:S(2)}) collective-permute-start(bf16[256,768]{1,0:T(8,128)(2,1)S(1)} %collective-permute-done.21), channel_id=1, source_target_pairs={{0,1},{1,2},{2,3},{3,0},{4,5},{5,6},{6,7},{7,4},{8,9},{9,10},{10,1... | collective-permute-start | bytes 1179656 | tf_op jit(solution)/shard_map/ppermute | solution.py:23
  495.1 93.1 %reduce-scatter.27.cloned.1.call-start = ((), (), s32[]{:S(2)}) async-start(), calls=%async_computation.21 | async-start | bytes 1966080 | tf_op jit(solution)/shard_map/reduce_scatter | solution.py:180
  506.4 112.3 %reduce-scatter.31.cloned.1.call-start = ((), (), s32[]{:S(2)}) async-start(), calls=%async_computation.23 | async-start | bytes 1966080 | tf_op jit(solution)/shard_map/reduce_scatter | solution.py:180
  511.8 152.8 %reduce-scatter.23.cloned.1.call-start = ((), (), s32[]{:S(2)}) async-start(), calls=%async_computation.19 | async-start | bytes 1966080 | tf_op jit(solution)/shard_map/reduce_scatter | solution.py:180
  516.8 162.9 %reduce-scatter.19.cloned.1.call-start = ((), (), s32[]{:S(2)}) async-start(), calls=%async_computation.17 | async-start | bytes 1966080 | tf_op jit(solution)/shard_map/reduce_scatter | solution.py:180
  521.4 232.0 %reduce-scatter.41.cloned.1.call-start = ((), (), s32[]{:S(2)}) async-start(), calls=%async_computation.28 | async-start | bytes 2654208 | tf_op jit(solution)/shard_map/reduce_scatter | solution.py:171
  528.6 297.8 %reduce-scatter.39.cloned.1.call-start = ((), (), s32[]{:S(2)}) async-start(), calls=%async_computation.27 | async-start | bytes 2654208 | tf_op jit(solution)/shard_map/reduce_scatter | solution.py:170
  535.4 357.3 %reduce-scatter.37.cloned.1.call-start = ((), (), s32[]{:S(2)}) async-start(), calls=%async_computation.26 | async-start | bytes 884736 | tf_op jit(solution)/shard_map/reduce_scatter | solution.py:168
  546.1 412.6 %reduce-scatter.35.cloned.1.call-start = ((), (), s32[]{:S(2)}) async-start(), calls=%async_computation.25 | async-start | bytes 884736 | tf_op jit(solution)/shard_map/reduce_scatter | solution.py:167
  558.3 466.7 %reduce-scatter.33.cloned.1.call-start = ((), (), s32[]{:S(2)}) async-start(), calls=%async_computation.24 | async-start | bytes 884736 | tf_op jit(solution)/shard_map/reduce_scatter | solution.py:166
  (188 other events, 2180.4 us)
Sparse Core Ops, SparseCore 0:
  165.2 29.0 reduce-scatter.16
  230.3 27.7 reduce-scatter.20
  324.7 34.0 reduce-scatter.28
  370.2 26.3 reduce-scatter.24
Sparse Core Ops, SparseCore 1:
  232.8 41.2 all-gather.2
  276.1 39.6 all-gather.4
  495.2 63.3 reduce-scatter.42
  561.2 27.0 reduce-scatter.26
  590.8 27.9 reduce-scatter.30
  621.3 27.9 reduce-scatter.22
  651.7 27.9 reduce-scatter.18
  683.6 69.7 reduce-scatter.40
  757.4 68.9 reduce-scatter.38
  830.2 62.4 reduce-scatter.36
  896.4 62.3 reduce-scatter.34
  962.7 62.3 reduce-scatter.32
